TPU v7x, 32 devices: a whole 2x2x4 slice. The times are simulated.
32 devices in a mesh: ctx: 16 (over z, y, x), tp: 2 (over core).
Axes of the slice: x: 2, y: 2, z: 4, core: 2. Of those that a mesh axis runs over, the one named last changes fastest.
Arguments:
- byte_states: bfloat16 [4096, 1024], P('ctx'), may hold values from -12 to 12, as said below
- patch_of_byte: int32 [4096], P('ctx'), may hold values from 0 to 125, as said below
- patch_first: int32 [16], replicated, may hold values from 0 to 991, as said below
- moved: int32 [2, 16], replicated, may hold values from 0 to 32, as said below
- w_qkv: bfloat16 [3, 1024, 2048], P(None, None, 'tp'), may hold values from -0.25 to 0.25, as said below
- d_attn: bfloat16 [1024, 2048], P('ctx', 'tp'), may hold values from -6 to 6
Outputs:
- attn_out: bfloat16 [1024, 2048], P('ctx', 'tp')
- byte_grad: bfloat16 [4096, 1024], P('ctx', 'tp')
Inputs may be any that keep to these rules, and one draw needn't show every extreme that they name: `patch_of_byte`: within each byte shard the numbers start at 0 and rise by 0 or 1 from byte to byte; a shard holds at most 126 patches, reached on some shard. `patch_first`: the sum of the patch counts of all earlier byte shards; shard 0 starts at 0. moved[0, 0] = 0 and moved[1, 15] = 0; every other entry is 1 to 32; every patch shard thereby receives exactly 64 patches, and the patch counts agree with patch_first and patch_of_byte. `w_qkv`: independent entries of order 1024 ** -0.5. `byte_states`: entries of order one.
All inputs are finite; a program needn't handle non-finite values.
Results may differ from a plain program's by a relative error of at most 0.011.
Values may be sent and summed in bfloat16 or wider, within the bound.
A program may use at most 64 MiB of HBM per device.

v0:
```python
import jax
import jax.numpy as jnp
from jax import lax
from jax.sharding import PartitionSpec as P

HD = 128


def extended_2(x, sides, width):
    for axis, dim in sides:
        peers, length = (lax.axis_size(axis), x.shape[dim])
        up = [(i, (i + 1) % peers) for i in range(peers - 1)]
        down = [(j, i) for i, j in up]
        last = lax.slice_in_dim(x, length - width, length, axis=dim)
        first = lax.slice_in_dim(x, 0, width, axis=dim)
        before = lax.ppermute(last, axis, up)
        after = lax.ppermute(first, axis, down)
        x = jnp.concatenate([before, x, after], axis=dim)
    return x


def pick_own(values, index):
    return lax.dynamic_index_in_dim(values, index, 0, keepdims=False)


def shards(byte_states, patch_of_byte, patch_first, moved, w_qkv, d_attn):
    ctx_index = lax.axis_index("ctx")
    n_ctx = lax.axis_size("ctx")
    rows = d_attn.shape[0]
    feats = d_attn.shape[1]
    heads = feats // HD
    capacity = 2 * rows
    total = rows * n_ctx
    scale = HD ** (-0.5)
    ends = jnp.concatenate([patch_first[1:], jnp.full((1,), total, jnp.int32)])
    counts = ends - patch_first
    lower_moves = moved[0]
    upper_moves = moved[1]
    zero_one = jnp.zeros((1,), jnp.int32)
    below_high = jnp.concatenate([zero_one, upper_moves[:-1]])
    above_low = jnp.concatenate([lower_moves[1:], zero_one])
    prev_first = jnp.concatenate([zero_one, patch_first[:-1]])
    prev_count = jnp.concatenate([zero_one, counts[:-1]])
    ranks = jnp.arange(rows, dtype=jnp.int32)[None, :]
    from_low = ranks < below_high[:, None]
    from_high = ranks >= (rows - above_low)[:, None]
    lower_local = prev_count[:, None] - below_high[:, None] + ranks
    own_local = lower_moves[:, None] + ranks - below_high[:, None]
    upper_local = ranks - (rows - above_low)[:, None]
    ids_all = jnp.where(
        from_low,
        prev_first[:, None] + lower_local,
        jnp.where(from_high, ends[:, None] + upper_local, patch_first[:, None] + own_local),
    )
    source_all = jnp.where(
        from_low,
        lower_local,
        jnp.where(from_high, 2 * capacity + upper_local, capacity + own_local),
    )
    wanted = pick_own(ids_all, ctx_index)
    source_rows = pick_own(source_all, ctx_index)
    key_place = ids_all.reshape(-1)
    slots = jnp.arange(capacity, dtype=jnp.int32)
    member = patch_of_byte[None, :] == slots[:, None]
    lengths = jnp.sum(member.astype(jnp.float32), axis=1)
    onehot = member.astype(jnp.bfloat16)
    part = byte_states.shape[1] // lax.axis_size("tp")
    source = lax.dynamic_slice_in_dim(byte_states, lax.axis_index("tp") * part, part, 1)
    pooled_local = (
        jnp.dot(onehot, source, preferred_element_type=jnp.float32)
        / jnp.maximum(lengths, 1.0)[:, None]
    ).astype(jnp.bfloat16)
    extended = extended_2(pooled_local, (("ctx", 0),), capacity)
    picker = (source_rows[:, None] == jnp.arange(3 * capacity, dtype=jnp.int32)[None, :]).astype(
        jnp.bfloat16
    )
    pooled = jnp.dot(picker, extended, preferred_element_type=jnp.float32).astype(jnp.bfloat16)
    pooled = lax.all_gather(pooled, "tp", axis=1, tiled=True)
    query = jnp.dot(pooled, w_qkv[0], preferred_element_type=jnp.float32).astype(jnp.bfloat16)
    keyed = jnp.dot(pooled, w_qkv[1], preferred_element_type=jnp.float32).astype(jnp.bfloat16)
    valued = jnp.dot(pooled, w_qkv[2], preferred_element_type=jnp.float32).astype(jnp.bfloat16)
    keys_all, values_all = (
        lax.all_gather(keyed, "ctx", axis=0, tiled=True),
        lax.all_gather(valued, "ctx", axis=0, tiled=True),
    )
    query3 = query.reshape(rows, heads, HD)
    keys3 = keys_all.reshape(total, heads, HD)
    values3 = values_all.reshape(total, heads, HD)
    causal = (wanted[:, None] >= key_place[None, :])[None, :, :]
    score = jnp.einsum("qhd,khd->hqk", query3, keys3, preferred_element_type=jnp.float32) * scale
    masked = jnp.where(causal, score, -jnp.inf)
    top = jnp.max(masked, axis=2, keepdims=True)
    lse = top + jnp.log(jnp.sum(jnp.exp(masked - top), axis=2, keepdims=True))
    prob = jnp.exp(jnp.where(causal, score - lse, -jnp.inf))
    probs = prob.astype(jnp.bfloat16)
    output3 = jnp.einsum("hqk,khd->qhd", probs, values3, preferred_element_type=jnp.float32).astype(
        jnp.bfloat16
    )
    attn_out = output3.reshape(rows, feats)
    grad3 = d_attn.reshape(rows, heads, HD)
    delta = jnp.sum(grad3.astype(jnp.float32) * output3.astype(jnp.float32), axis=2)
    dprob = jnp.einsum("qhd,khd->hqk", grad3, values3, preferred_element_type=jnp.float32)
    dscore = (prob * (dprob - jnp.transpose(delta)[:, :, None])).astype(jnp.bfloat16)
    d_query = (
        jnp.einsum("hqk,khd->qhd", dscore, keys3, preferred_element_type=jnp.float32) * scale
    ).astype(jnp.bfloat16)
    lse_rows = jnp.transpose(lse[:, :, 0])
    lse_all, delta_all = (
        lax.all_gather(lse_rows, "ctx", axis=0, tiled=True),
        lax.all_gather(delta, "ctx", axis=0, tiled=True),
    )
    own_keys = keyed.reshape(rows, heads, HD)
    own_values = valued.reshape(rows, heads, HD)
    q_piece = lax.all_gather(query, "ctx", axis=0, tiled=True)
    g_piece = lax.all_gather(d_attn, "ctx", axis=0, tiled=True)
    count = q_piece.shape[0]
    q_three = q_piece.reshape(count, heads, HD)
    g_three = g_piece.reshape(count, heads, HD)
    lse_piece = jnp.transpose(lse_all)
    delta_piece = jnp.transpose(delta_all)
    allowed = (key_place[:, None] >= wanted[None, :])[None, :, :]
    part_score = (
        jnp.einsum("qhd,khd->hqk", q_three, own_keys, preferred_element_type=jnp.float32) * scale
    )
    part_prob = jnp.exp(jnp.where(allowed, part_score - lse_piece[:, :, None], -jnp.inf))
    part_probs = part_prob.astype(jnp.bfloat16)
    d_value_sum = jnp.einsum(
        "hqk,qhd->khd", part_probs, g_three, preferred_element_type=jnp.float32
    )
    part_dprob = jnp.einsum("qhd,khd->hqk", g_three, own_values, preferred_element_type=jnp.float32)
    part_dscore = (part_prob * (part_dprob - delta_piece[:, :, None])).astype(jnp.bfloat16)
    d_key_sum = (
        jnp.einsum("hqk,qhd->khd", part_dscore, q_three, preferred_element_type=jnp.float32) * scale
    )
    d_key_sum, d_value_sum = (d_key_sum, d_value_sum)
    d_key = d_key_sum.astype(jnp.bfloat16).reshape(rows, feats)
    d_value = d_value_sum.astype(jnp.bfloat16).reshape(rows, feats)
    d_query = d_query.reshape(rows, feats)
    contract = (((1,), (1,)), ((), ()))
    partial_value = lax.dot_general(d_query, w_qkv[0], contract, preferred_element_type=jnp.float32)
    partial_value = partial_value + lax.dot_general(
        d_key, w_qkv[1], contract, preferred_element_type=jnp.float32
    )
    partial_value = partial_value + lax.dot_general(
        d_value, w_qkv[2], contract, preferred_element_type=jnp.float32
    )
    d_pooled = lax.psum_scatter(partial_value, "tp", scatter_dimension=1, tiled=True).astype(
        jnp.bfloat16
    )
    returned = extended_2(d_pooled, (("ctx", 0),), rows)
    my_count = pick_own(counts, ctx_index)
    my_low = pick_own(lower_moves, ctx_index)
    my_high = pick_own(upper_moves, ctx_index)
    my_below = pick_own(below_high, ctx_index)
    target = jnp.where(
        patch_of_byte < my_low,
        rows - my_low + patch_of_byte,
        jnp.where(
            patch_of_byte >= my_count - my_high,
            2 * rows + patch_of_byte - (my_count - my_high),
            rows + my_below + patch_of_byte - my_low,
        ),
    )
    chooser = (target[:, None] == jnp.arange(3 * rows, dtype=jnp.int32)[None, :]).astype(
        jnp.bfloat16
    )
    spread_back = jnp.dot(chooser, returned, preferred_element_type=jnp.float32)
    byte_lengths = jnp.sum(jnp.where(member, lengths[:, None], 0.0), axis=0)
    byte_grad = (spread_back / byte_lengths[:, None]).astype(jnp.bfloat16)
    return (attn_out, byte_grad)


def solution(mesh):
    placed = (P("ctx", None), P("ctx"), P(), P(), P(None, None, "tp"), P("ctx", "tp"))
    return jax.shard_map(
        shards,
        mesh=mesh,
        in_specs=placed,
        out_specs=(P("ctx", "tp"), P("ctx", "tp")),
        check_vma=False,
    )
```

profile of v0, /device:TPU:6, one launch (start us, length us, event | category | flops | bytes accessed | tf_op | source)
XLA Modules:
  0.0 305.7 jit_solution(10949627991634043434)
XLA Ops:
  7.2 0.7 all-gather.13.cloned.1.call-update
  8.0 0.8 convert_reduce_fusion
  8.8 0.9 fusion.56
  9.7 3.4 %collective-permute-start = (bf16[128,512]{1,0:T(8,128)(2,1)S(1)}, bf16[128,512]{1,0:T(8,128)(2,1)S(1)}, u32[]{:S(2)}, u32[]{:S(2)}) collective-permute-start(bf16[128,512]{1,0:T(8,128)(2,1)S(1)} %fusion.56), channel_id=1, source_target_pairs={{0,2},{2,4},{4,6},{6,8},{8,10},{10,12},{12,14},{14,16},{16,18},{18... | collective-permute-start | bytes 393224 | tf_op jit(solution)/shard_map/ppermute | solution.py:16
  13.1 2.4 collective-permute-start.1
  15.5 0.8 slice_bitcast_fusion.1
  16.4 0.8 fusion.133
  17.2 0.7 pad_add_fusion.3
  18.0 0.8 fusion.132
  19.2 1.2 dynamic-slice.3
  20.4 0.6 dynamic-slice.4
  21.0 0.6 dynamic-slice.2
  21.6 1.9 select_bitcast_fusion
  23.5 0.2 convolution_convert_fusion.1
  23.8 1.9 all_gather.21
  25.7 2.7 fusion.66
  28.5 2.7 fusion.60
  31.3 2.7 fusion.63
  35.4 36.0 %all-gather.13.cloned.1.call-done = bf16[1024,1024]{1,0:T(8,128)(2,1)} async-done(((bf16[64,1024]{1,0:T(8,128)(2,1)}), bf16[1024,1024]{1,0:T(8,128)(2,1)}) %all-gather.13.cloned.1.call-update) | async-done | bytes 2097168 | tf_op jit(solution)/shard_map/all_gather | solution.py:115
  71.4 2.9 copy.61
  74.3 59.7 %all-gather.9.cloned.1.call-done = bf16[1024,1024]{1,0:T(8,128)(2,1)} async-done(((bf16[64,1024]{1,0:T(8,128)(2,1)}), bf16[1024,1024]{1,0:T(8,128)(2,1)}) %all-gather.9.cloned.1.call-update) | async-done | bytes 2097168 | tf_op jit(solution)/shard_map/all_gather | solution.py:83
  134.0 2.6 select_reduce_fusion
  136.6 1.3 copy-done.2
  137.9 0.6 exponential_reduce_fusion
  138.5 33.8 %all-gather = f32[16,64,8]{1,2,0:T(8,128)S(1)} all-gather(f32[1,64,8]{1,2,0:T(8,128)S(1)} %bitcast.202), channel_id=1, replica_groups=mesh['ctx'=16,'tp'=2] {'ctx'}, dimensions={0}, use_global_device_ids=true | all-gather | bytes 34816 | tf_op jit(solution)/shard_map/all_gather | solution.py:109
  172.4 23.7 %all-gather.7.cloned.1.call-done = bf16[1024,1024]{1,0:T(8,128)(2,1)} async-done(((bf16[64,1024]{1,0:T(8,128)(2,1)}), bf16[1024,1024]{1,0:T(8,128)(2,1)}) %all-gather.7.cloned.1.call-update) | async-done | bytes 2097168 | tf_op jit(solution)/shard_map/all_gather | solution.py:84
  196.2 3.8 %multiply_reduce_fusion = (f32[64,8]{0,1:T(8,128)S(1)}, bf16[8,128,64]{1,2,0:T(8,128)(2,1)}) fusion(f32[8,64,1024]{2,1,0:T(8,128)} %copy-done.2, f32[8,64]{1,0:T(8,128)S(1)} %log_add_fusion, pred[64,1024]{1,0:T(8,128)(4,1)S(1)} %broadcast_compare_fusion.1, bf16[1024,1024]{1,0:T(8,128)(2,1)} %all-gather.7.cloned.1.call-done, bf16[64,1024]{1,0:T(8,128)(2,1)S(1)} %copy-done.6), kind=kOutput, calls=%fused_computation.75 | convolution fusion | flops 136642048 | bytes 4526080 | tf_op jit(solution)/shard_map/hqk,khd->qhd/dot_general | solution.py:96
  200.0 33.9 %all-gather.1 = f32[16,64,8]{1,2,0:T(8,128)S(1)} all-gather(f32[1,64,8]{1,2,0:T(8,128)S(1)} %bitcast.203), channel_id=1, replica_groups=mesh['ctx'=16,'tp'=2] {'ctx'}, dimensions={0}, use_global_device_ids=true | all-gather | bytes 34816 | tf_op jit(solution)/shard_map/all_gather | solution.py:110
  233.9 24.8 %all-gather.11.cloned.1.call-done = bf16[1024,1024]{1,0:T(8,128)(2,1)} async-done(((bf16[64,1024]{1,0:T(8,128)(2,1)}), bf16[1024,1024]{1,0:T(8,128)(2,1)}) %all-gather.11.cloned.1.call-update) | async-done | bytes 2097168 | tf_op jit(solution)/shard_map/all_gather | solution.py:114
  258.7 2.7 select_exponential_fusion
  261.4 0.9 fusion.78
  262.3 0.5 copy-done.1
  262.8 3.3 %fusion.75 = bf16[8,8,8,128]{3,2,1,0:T(8,128)(2,1)S(1)} fusion(f32[8,1024,64]{1,2,0:T(8,128)} %copy-done.1, bf16[1024,8,128]{0,2,1:T(8,128)(2,1)S(1)} %bitcast.199, f32[8,1024]{1,0:T(8,128)S(1)} %bitcast.200, bf16[1024,1024]{1,0:T(8,128)(2,1)} %all-gather.11.cloned.1.call-done, bf16[64,1024]{1,0:T(8,128)(2,1)S(1)} %copy-done.4), kind=kOutput, calls=%fused_computation.60 | convolution fusion | flops 270139392 | bytes 6586368 | tf_op jit(solution)/shard_map/hqk,qhd->khd/dot_general | solution.py:133
  266.1 2.5 fusion.14
  268.6 4.0 %fusion.79 = bf16[8,8,8,128]{3,2,1,0:T(8,128)(2,1)S(1)} fusion(f32[8,64,1024]{2,1,0:T(8,128)S(1)} %copy-done.3, f32[8,64]{1,0:T(8,128)S(1)} %bitcast.204, f32[8,64]{1,0:T(8,128)S(1)} %log_add_fusion, pred[64,1024]{1,0:T(8,128)(4,1)S(1)} %broadcast_compare_fusion.1, bf16[1024,1024]{1,0:T(8,128)(2,1)} %all-gather.7.cloned.1.call-done, ...), kind=kOutput, calls=%fused_computation.62 | convolution fusion | flops 271712256 | bytes 6623232 | tf_op jit(solution)/shard_map/hqk,khd->qhd/dot_general | solution.py:105
  272.6 2.4 fusion.47
  275.0 3.1 %fusion.44 = f32[64,1024]{1,0:T(8,128)} fusion(f32[64,1024]{1,0:T(8,128)S(1)} %fusion.47, bf16[3,1024,1024]{2,1,0:T(8,128)(2,1)} %param.10, bf16[8,8,8,128]{3,2,1,0:T(8,128)(2,1)S(1)} %fusion.78), kind=kOutput, calls=%fused_computation.47 | convolution fusion | flops 134283264 | bytes 2752512 | tf_op jit(solution)/shard_map/dot_general | solution.py:144
  278.1 0.6 dynamic_slice.27
  278.7 0.6 dynamic_slice.29
  279.3 0.7 constant_dynamic-slice_fusion.3
  282.7 0.7 compare_select_fusion.1
  283.4 2.6 reduce-scatter.2.cloned.1.call-done
  285.9 0.9 convert_element_type.89
  286.9 3.4 %collective-permute-start.2 = (bf16[64,512]{1,0:T(8,128)(2,1)S(1)}, bf16[64,512]{1,0:T(8,128)(2,1)S(1)}, u32[]{:S(2)}, u32[]{:S(2)}) collective-permute-start(bf16[64,512]{1,0:T(8,128)(2,1)S(1)} %convert_element_type.89), channel_id=1, source_target_pairs={{0,2},{2,4},{4,6},{6,8},{8,10},{10,12},{12,14},{14,16},{16,18},{18... | collective-permute-start | bytes 196616 | tf_op jit(solution)/shard_map/ppermute | solution.py:16
  290.2 2.5 collective-permute-start.3
  292.7 0.7 copy_bitcast_fusion
  293.4 4.8 %collective-permute-done.3 = bf16[64,512]{1,0:T(8,128)(2,1)S(1)} collective-permute-done((bf16[64,512]{1,0:T(8,128)(2,1)S(1)}, bf16[64,512]{1,0:T(8,128)(2,1)S(1)}, u32[]{:S(2)}, u32[]{:S(2)}) %collective-permute-start.3) | collective-permute-done | bytes 65568 | tf_op jit(solution)/shard_map/ppermute | solution.py:17
  298.2 1.0 fusion.43
  (65 shorter events, 2.5 us)
Async XLA Ops:
  7.2 1.6 copy-start
  7.2 64.3 %all-gather.13.cloned.1.call-start = ((), (), s32[]{:S(2)}) async-start(), calls=%async_computation.4 | async-start | bytes 2228224 | tf_op jit(solution)/shard_map/all_gather | solution.py:115
  7.9 126.1 %all-gather.9.cloned.1.call-start = ((), (), s32[]{:S(2)}) async-start(), calls=%async_computation.2 | async-start | bytes 2228224 | tf_op jit(solution)/shard_map/all_gather | solution.py:83
  9.7 13.9 %collective-permute-start = (bf16[128,512]{1,0:T(8,128)(2,1)S(1)}, bf16[128,512]{1,0:T(8,128)(2,1)S(1)}, u32[]{:S(2)}, u32[]{:S(2)}) collective-permute-start(bf16[128,512]{1,0:T(8,128)(2,1)S(1)} %fusion.56), channel_id=1, source_target_pairs={{0,2},{2,4},{4,6},{6,8},{8,10},{10,12},{12,14},{14,16},{16,18},{18... | collective-permute-start | bytes 393224 | tf_op jit(solution)/shard_map/ppermute | solution.py:16
  13.1 10.5 %collective-permute-start.1 = (bf16[128,512]{1,0:T(8,128)(2,1)S(1)}, bf16[128,512]{1,0:T(8,128)(2,1)S(1)}, u32[]{:S(2)}, u32[]{:S(2)}) collective-permute-start(bf16[128,512]{1,0:T(8,128)(2,1)S(1)} %fusion.56), channel_id=1, source_target_pairs={{2,0},{4,2},{6,4},{8,6},{10,8},{12,10},{14,12},{16,14},{18,16},{20... | collective-permute-start | bytes 393224 | tf_op jit(solution)/shard_map/ppermute | solution.py:17
  28.4 167.7 %all-gather.7.cloned.1.call-start = ((), (), s32[]{:S(2)}) async-start(), calls=%async_computation.1 | async-start | bytes 2228224 | tf_op jit(solution)/shard_map/all_gather | solution.py:84
  31.2 3.7 %copy-start.9 = (s32[16]{0:T(128)S(1)}, s32[16]{0:T(128)}, u32[]{:S(2)}) copy-start(s32[16]{0:T(128)} %param.8) | copy-start | bytes 196
  31.2 227.5 %all-gather.11.cloned.1.call-start = ((), (), s32[]{:S(2)}) async-start(), calls=%async_computation.3 | async-start | bytes 2228224 | tf_op jit(solution)/shard_map/all_gather | solution.py:114
  34.0 251.9 %reduce-scatter.2.cloned.1.call-start = ((), (), s32[]{:S(2)}) async-start(), calls=%async_computation.5 | async-start | bytes 393216 | tf_op jit(solution)/shard_map/reduce_scatter | solution.py:147
  35.4 98.6 %copy-start.5 = (bf16[64,1024]{1,0:T(8,128)(2,1)S(1)}, bf16[64,1024]{1,0:T(8,128)(2,1)}, u32[]{:S(2)}) copy-start(bf16[64,1024]{1,0:T(8,128)(2,1)} %fusion.63) | copy-start | bytes 393220
  136.6 1.4 copy-start.2
  136.6 59.6 %copy-start.6 = (bf16[64,1024]{1,0:T(8,128)(2,1)S(1)}, bf16[64,1024]{1,0:T(8,128)(2,1)}, u32[]{:S(2)}) copy-start(bf16[64,1024]{1,0:T(8,128)(2,1)} %param.11) | copy-start | bytes 393220
  172.4 86.3 %copy-start.7 = (bf16[64,1024]{1,0:T(8,128)(2,1)S(1)}, bf16[64,1024]{1,0:T(8,128)(2,1)}, u32[]{:S(2)}) copy-start(bf16[64,1024]{1,0:T(8,128)(2,1)} %fusion.66) | copy-start | bytes 393220
  261.4 1.4 copy-start.1
  261.4 1.4 copy-start.4
  266.1 2.5 copy-start.3
  275.0 7.6 %copy-start.10 = (s32[256]{0:T(256)S(1)}, s32[256]{0:T(256)}, u32[]{:S(2)}) copy-start(s32[256]{0:T(256)} %param.7) | copy-start | bytes 3076
  275.0 17.7 %copy-start.8 = (bf16[8,128,64]{1,2,0:T(8,128)(2,1)S(1)}, bf16[8,128,64]{1,2,0:T(8,128)(2,1)}, u32[]{:S(2)}) copy-start(bf16[8,128,64]{1,2,0:T(8,128)(2,1)} %get-tuple-element.18) | copy-start | bytes 393220
  286.9 6.5 %collective-permute-start.2 = (bf16[64,512]{1,0:T(8,128)(2,1)S(1)}, bf16[64,512]{1,0:T(8,128)(2,1)S(1)}, u32[]{:S(2)}, u32[]{:S(2)}) collective-permute-start(bf16[64,512]{1,0:T(8,128)(2,1)S(1)} %convert_element_type.89), channel_id=1, source_target_pairs={{0,2},{2,4},{4,6},{6,8},{8,10},{10,12},{12,14},{14,16},{16,18},{18... | collective-permute-start | bytes 196616 | tf_op jit(solution)/shard_map/ppermute | solution.py:16
  290.2 8.0 %collective-permute-start.3 = (bf16[64,512]{1,0:T(8,128)(2,1)S(1)}, bf16[64,512]{1,0:T(8,128)(2,1)S(1)}, u32[]{:S(2)}, u32[]{:S(2)}) collective-permute-start(bf16[64,512]{1,0:T(8,128)(2,1)S(1)} %convert_element_type.89), channel_id=1, source_target_pairs={{2,0},{4,2},{6,4},{8,6},{10,8},{12,10},{14,12},{16,14},{18,16},{20... | collective-permute-start | bytes 196616 | tf_op jit(solution)/shard_map/ppermute | solution.py:17
Sparse Core Ops, SparseCore 0:
  10.8 60.6 all-gather.12
  74.8 59.1 all-gather.8
  136.8 59.3 all-gather.6
  199.4 59.2 all-gather.10
  278.3 7.6 reduce-scatter.1
where the time goes:
time: 306 us
  waiting for transfers between devices  152 us (50%)
  blocking collectives  69.5 us (23%)
  matrix products  35.5 us (12%)
  between operations  16.7 us (5%)
  local copies, waits for them, and re-layouts  13.3 us (4%)
  starting transfers between devices  11.9 us (4%)
  other arithmetic  6.49 us (2%)
    all_gather x1, waiting for transfers between devices, shards(): lax.all_gather(keyed, 'ctx', axis=0, tiled=True)  59.7 us
    all_gather x1, waiting for transfers between devices, shards(): g_piece = lax.all_gather(d_attn, 'ctx', axis=0, tiled=True)  36 us
    all_gather x1, blocking collectives, shards(): lax.all_gather(delta, 'ctx', axis=0, tiled=True)  33.9 us
    all_gather x1, blocking collectives, shards(): lax.all_gather(lse_rows, 'ctx', axis=0, tiled=True)  33.8 us
    all_gather x1, waiting for transfers between devices, shards(): q_piece = lax.all_gather(query, 'ctx', axis=0, tiled=True)  24.8 us
    all_gather x1, waiting for transfers between devices, shards(): lax.all_gather(valued, 'ctx', axis=0, tiled=True)  23.7 us
    ppermute x2, starting transfers between devices, extended_2(): before = lax.ppermute(last, axis, up)  6.77 us
  transfers between devices with their start and end apart: 9, of which 6 were waited for; matrix products, arithmetic and copies ran while one was open for 11% of the time, Pallas kernels for 0%

commit v1 on v0

--- a/solution.py
+++ b/solution.py
@@ -4,6 +4,24 @@
 from jax.sharding import PartitionSpec as P
 
 HD = 128
+
+
+def gather_around(shard, axis, dim):
+    ways, here, step = (lax.axis_size(axis), lax.axis_index(axis), shard.shape[dim])
+    shape = [n * ways if d == dim else n for d, n in enumerate(shard.shape)]
+    full = lax.dynamic_update_slice_in_dim(
+        jnp.zeros(shape, shard.dtype), shard, here * step, axis=dim
+    )
+    going_up = going_down = shard
+    for far in range(1, ways // 2 + 1):
+        going_up = lax.ppermute(going_up, axis, [(d, (d + 1) % ways) for d in range(ways)])
+        full = lax.dynamic_update_slice_in_dim(full, going_up, (here - far) % ways * step, axis=dim)
+        if 2 * far < ways:
+            going_down = lax.ppermute(going_down, axis, [(d, (d - 1) % ways) for d in range(ways)])
+            full = lax.dynamic_update_slice_in_dim(
+                full, going_down, (here + far) % ways * step, axis=dim
+            )
+    return full
 
 
 def extended_2(x, sides, width):
@@ -81,7 +99,7 @@
     valued = jnp.dot(pooled, w_qkv[2], preferred_element_type=jnp.float32).astype(jnp.bfloat16)
     keys_all, values_all = (
         lax.all_gather(keyed, "ctx", axis=0, tiled=True),
-        lax.all_gather(valued, "ctx", axis=0, tiled=True),
+        gather_around(valued, "ctx", 0),
     )
     query3 = query.reshape(rows, heads, HD)
     keys3 = keys_all.reshape(total, heads, HD)

time: 306 us -> 277 us (0.905)
  waiting for transfers between devices: 152 us -> 53 us
  local copies, waits for them, and re-layouts: 13.3 us -> 48.1 us
  starting transfers between devices: 11.9 us -> 44 us
  blocking collectives: 69.5 us -> 75.3 us
  matrix products: 35.5 us -> 32.4 us
    all_gather x1, waiting for transfers between devices: 59.7 us -> 17.1 us  [shards(): lax.all_gather(keyed, 'ctx', axis=0, tiled=True)]
    all_gather x1, waiting for transfers between devices: 36 us -> 0.01 us  [shards(): g_piece = lax.all_gather(d_attn, 'ctx', axis=0, tiled=True)]
    ppermute x0 -> x15, starting transfers between devices: none -> 32.1 us  [the longest x8 29.8 us: gather_around(): lax.ppermute(going_up, axis, [(d, (d + 1) % ways) for d in range(ways)])]
    ppermute x0 -> x15, waiting for transfers between devices: none -> 26.6 us  [the longest x8 19.4 us: gather_around(): lax.ppermute(going_up, axis, [(d, (d + 1) % ways) for d in range(ways)])]
    dynamic_update_slice x0 -> x16, local copies, waits for them, and re-layouts: none -> 25.6 us  [the longest x8 12.5 us: gather_around(): lax.dynamic_update_slice_in_dim(full, going_up, (here - far) % ways * ste...]
    all_gather x1, waiting for transfers between devices: 24.8 us -> 0.01 us  [shards(): q_piece = lax.all_gather(query, 'ctx', axis=0, tiled=True)]
    all_gather x1 -> x0, waiting for transfers between devices: 23.7 us -> none  [shards(): lax.all_gather(valued, 'ctx', axis=0, tiled=True)]
    ppermute x0 -> x15, local copies, waits for them, and re-layouts: none -> 6.14 us  [the longest x8 3.15 us: gather_around(): lax.ppermute(going_up, axis, [(d, (d + 1) % ways) for d in range(ways)])]
  transfers between devices with their start and end apart: 9 -> 23, of which waited for: 6 -> 13; matrix products, arithmetic and copies ran while one was open for 11% -> 23% of each run, Pallas kernels for 0% -> 0%
where the time goes in v1:
time: 277 us; the launch traced here: 276 us
  blocking collectives  75.3 us (27%)
  waiting for transfers between devices  53 us (19%)
  local copies, waits for them, and re-layouts  48.1 us (17%)
  starting transfers between devices  44 us (16%)
  matrix products  32.4 us (12%)
  between operations  17.1 us (6%)
  other arithmetic  6.39 us (2%)
    all_gather x1, blocking collectives, shards(): lax.all_gather(lse_rows, 'ctx', axis=0, tiled=True)  39.5 us
    all_gather x1, blocking collectives, shards(): lax.all_gather(delta, 'ctx', axis=0, tiled=True)  33.9 us
    ppermute x8, starting transfers between devices, gather_around(): lax.ppermute(going_up, axis, [(d, (d + 1) % ways) for d in range(ways)])  29.8 us
    ppermute x8, waiting for transfers between devices, gather_around(): lax.ppermute(going_up, axis, [(d, (d + 1) % ways) for d in range(ways)])  19.4 us
    all_gather x1, waiting for transfers between devices, shards(): lax.all_gather(keyed, 'ctx', axis=0, tiled=True)  17.1 us
    dynamic_update_slice x8, local copies, waits for them, and re-layouts, gather_around(): lax.dynamic_update_slice_in_dim(full, going_up, (here - far) % ways * ste...  12.5 us
    dynamic_update_slice x7, local copies, waits for them, and re-layouts, gather_around(): lax.dynamic_update_slice_in_dim(full, going_down, (here + far) % ways * s...  11.1 us
    ppermute x7, waiting for transfers between devices, gather_around(): lax.ppermute(going_down, axis, [(d, (d - 1) % ways) for d in range(ways)])  7.2 us
  transfers between devices with their start and end apart: 23, of which 13 were waited for; matrix products, arithmetic and copies ran while one was open for 23% of the time, Pallas kernels for 0%

profile of v1, /device:TPU:6, one launch (start us, length us, event | category | flops | bytes accessed | tf_op | source)
XLA Modules:
  0.0 276.3 jit_solution(8172281466722485719)
XLA Ops:
  9.7 3.4 %collective-permute-start = (bf16[128,512]{1,0:T(8,128)(2,1)S(1)}, bf16[128,512]{1,0:T(8,128)(2,1)S(1)}, u32[]{:S(2)}, u32[]{:S(2)}) collective-permute-start(bf16[128,512]{1,0:T(8,128)(2,1)S(1)} %fusion.48), channel_id=1, source_target_pairs={{0,2},{2,4},{4,6},{6,8},{8,10},{10,12},{12,14},{14,16},{16,18},{18... | collective-permute-start | bytes 393224 | tf_op jit(solution)/shard_map/ppermute | solution.py:34
  13.1 2.4 collective-permute-start.1
  22.2 2.0 select_bitcast_fusion
  24.5 1.9 all_gather.18
  26.4 2.7 fusion.58
  29.2 2.7 fusion.55
  32.0 2.1 fusion.52
  34.1 3.3 %collective-permute-start.2 = (bf16[64,1024]{1,0:T(8,128)(2,1)S(1)}, bf16[64,1024]{1,0:T(8,128)(2,1)S(1)}, u32[]{:S(2)}, u32[]{:S(2)}) collective-permute-start(bf16[64,1024]{1,0:T(8,128)(2,1)S(1)} %fusion.52), channel_id=1, source_target_pairs={{0,2},{2,4},{4,6},{6,8},{8,10},{10,12},{12,14},{14,16},{16,18},{18... | collective-permute-start | bytes 393224 | tf_op jit(solution)/shard_map/ppermute | solution.py:17
  37.4 5.2 %collective-permute-done.2 = bf16[64,1024]{1,0:T(8,128)(2,1)S(1)} collective-permute-done((bf16[64,1024]{1,0:T(8,128)(2,1)S(1)}, bf16[64,1024]{1,0:T(8,128)(2,1)S(1)}, u32[]{:S(2)}, u32[]{:S(2)}) %collective-permute-start.2) | collective-permute-done | bytes 131104 | tf_op jit(solution)/shard_map/ppermute | solution.py:17
  42.6 3.6 %collective-permute-start.4 = (bf16[64,1024]{1,0:T(8,128)(2,1)S(1)}, bf16[64,1024]{1,0:T(8,128)(2,1)S(1)}, u32[]{:S(2)}, u32[]{:S(2)}) collective-permute-start(bf16[64,1024]{1,0:T(8,128)(2,1)S(1)} %collective-permute-done.2), channel_id=1, source_target_pairs={{0,2},{2,4},{4,6},{6,8},{8,10},{10,12},{12,14},{14,16},{16,18},{18... | collective-permute-start | bytes 393224 | tf_op jit(solution)/shard_map/ppermute | solution.py:17
  46.3 2.3 collective-permute-start.5
  48.5 2.4 collective-permute-done.4
  50.9 4.3 %collective-permute-start.6 = (bf16[64,1024]{1,0:T(8,128)(2,1)S(1)}, bf16[64,1024]{1,0:T(8,128)(2,1)S(1)}, u32[]{:S(2)}, u32[]{:S(2)}) collective-permute-start(bf16[64,1024]{1,0:T(8,128)(2,1)S(1)} %collective-permute-done.4), channel_id=1, source_target_pairs={{0,2},{2,4},{4,6},{6,8},{8,10},{10,12},{12,14},{14,16},{16,18},{18... | collective-permute-start | bytes 393224 | tf_op jit(solution)/shard_map/ppermute | solution.py:17
  55.2 2.5 collective-permute-done.6
  57.7 4.2 %collective-permute-start.8 = (bf16[64,1024]{1,0:T(8,128)(2,1)S(1)}, bf16[64,1024]{1,0:T(8,128)(2,1)S(1)}, u32[]{:S(2)}, u32[]{:S(2)}) collective-permute-start(bf16[64,1024]{1,0:T(8,128)(2,1)S(1)} %collective-permute-done.6), channel_id=1, source_target_pairs={{0,2},{2,4},{4,6},{6,8},{8,10},{10,12},{12,14},{14,16},{16,18},{18... | collective-permute-start | bytes 393224 | tf_op jit(solution)/shard_map/ppermute | solution.py:17
  62.5 5.1 %collective-permute-done.8 = bf16[64,1024]{1,0:T(8,128)(2,1)S(1)} collective-permute-done((bf16[64,1024]{1,0:T(8,128)(2,1)S(1)}, bf16[64,1024]{1,0:T(8,128)(2,1)S(1)}, u32[]{:S(2)}, u32[]{:S(2)}) %collective-permute-start.8) | collective-permute-done | bytes 131104 | tf_op jit(solution)/shard_map/ppermute | solution.py:17
  67.7 4.3 %collective-permute-start.10 = (bf16[64,1024]{1,0:T(8,128)(2,1)S(1)}, bf16[64,1024]{1,0:T(8,128)(2,1)S(1)}, u32[]{:S(2)}, u32[]{:S(2)}) collective-permute-start(bf16[64,1024]{1,0:T(8,128)(2,1)S(1)} %collective-permute-done.8), channel_id=1, source_target_pairs={{0,2},{2,4},{4,6},{6,8},{8,10},{10,12},{12,14},{14,16},{16,18},{18... | collective-permute-start | bytes 393224 | tf_op jit(solution)/shard_map/ppermute | solution.py:17
  73.1 3.3 %collective-permute-done.10 = bf16[64,1024]{1,0:T(8,128)(2,1)S(1)} collective-permute-done((bf16[64,1024]{1,0:T(8,128)(2,1)S(1)}, bf16[64,1024]{1,0:T(8,128)(2,1)S(1)}, u32[]{:S(2)}, u32[]{:S(2)}) %collective-permute-start.10) | collective-permute-done | bytes 131104 | tf_op jit(solution)/shard_map/ppermute | solution.py:17
  76.4 3.2 %collective-permute-start.12 = (bf16[64,1024]{1,0:T(8,128)(2,1)S(1)}, bf16[64,1024]{1,0:T(8,128)(2,1)S(1)}, u32[]{:S(2)}, u32[]{:S(2)}) collective-permute-start(bf16[64,1024]{1,0:T(8,128)(2,1)S(1)} %collective-permute-done.10), channel_id=1, source_target_pairs={{0,2},{2,4},{4,6},{6,8},{8,10},{10,12},{12,14},{14,16},{16,18},{18... | collective-permute-start | bytes 393224 | tf_op jit(solution)/shard_map/ppermute | solution.py:17
  79.7 2.9 %collective-permute-done.11 = bf16[64,1024]{1,0:T(8,128)(2,1)S(1)} collective-permute-done((bf16[64,1024]{1,0:T(8,128)(2,1)S(1)}, bf16[64,1024]{1,0:T(8,128)(2,1)S(1)}, u32[]{:S(2)}, u32[]{:S(2)}) %collective-permute-start.11) | collective-permute-done | bytes 131104 | tf_op jit(solution)/shard_map/ppermute | solution.py:20
  82.7 3.7 %collective-permute-start.14 = (bf16[64,1024]{1,0:T(8,128)(2,1)S(1)}, bf16[64,1024]{1,0:T(8,128)(2,1)}, u32[]{:S(2)}, u32[]{:S(2)}) collective-permute-start(bf16[64,1024]{1,0:T(8,128)(2,1)S(1)} %collective-permute-done.12), channel_id=1, source_target_pairs={{0,2},{2,4},{4,6},{6,8},{8,10},{10,12},{12,14},{14,16},{16,18},{18... | collective-permute-start | bytes 393224 | tf_op jit(solution)/shard_map/ppermute | solution.py:17
  86.5 3.7 %collective-permute-done.13 = bf16[64,1024]{1,0:T(8,128)(2,1)} collective-permute-done((bf16[64,1024]{1,0:T(8,128)(2,1)S(1)}, bf16[64,1024]{1,0:T(8,128)(2,1)}, u32[]{:S(2)}, u32[]{:S(2)}) %collective-permute-start.13) | collective-permute-done | bytes 131104 | tf_op jit(solution)/shard_map/ppermute | solution.py:20
  91.0 3.1 %collective-permute-start.16 = (bf16[64,1024]{1,0:T(8,128)(2,1)}, bf16[64,1024]{1,0:T(8,128)(2,1)}, u32[]{:S(2)}, u32[]{:S(2)}) collective-permute-start(bf16[64,1024]{1,0:T(8,128)(2,1)} %collective-permute-done.14), channel_id=1, source_target_pairs={{0,2},{2,4},{4,6},{6,8},{8,10},{10,12},{12,14},{14,16},{16,18},{18... | collective-permute-start | bytes 393224 | tf_op jit(solution)/shard_map/ppermute | solution.py:17
  94.7 2.0 dynamic_update_slice.48
  99.7 2.0 dynamic_update_slice.51
  101.9 2.0 dynamic_update_slice.52
  107.0 1.8 dynamic_update_slice.55
  109.0 2.0 dynamic_update_slice.56
  113.8 2.0 dynamic_update_slice.59
  116.9 2.2 dynamic_update_slice.60
  124.8 2.0 dynamic_update_slice.63
  128.3 2.9 %copy.108 = bf16[1024,1024]{0,1:T(8,128)(2,1)S(1)} copy(bf16[1024,1024]{1,0:T(8,128)(2,1)} %all-gather.10.cloned.1.call-done) | data formatting | bytes 4194304 | tf_op jit(solution)/shard_map/all_gather | solution.py:133
  131.2 17.1 %all-gather.6.cloned.1.call-done = bf16[1024,1024]{1,0:T(8,128)(2,1)} async-done(((bf16[64,1024]{1,0:T(8,128)(2,1)}), bf16[1024,1024]{1,0:T(8,128)(2,1)}) %all-gather.6.cloned.1.call-update) | async-done | bytes 2097168 | tf_op jit(solution)/shard_map/all_gather | solution.py:101
  148.3 2.6 select_reduce_fusion
  151.5 1.7 copy-done.5
  153.3 1.7 multiply_reduce_fusion
  154.9 33.9 %all-gather.1 = f32[16,64,8]{1,2,0:T(8,128)S(1)} all-gather(f32[1,64,8]{1,2,0:T(8,128)S(1)} %bitcast.187), channel_id=1, replica_groups=mesh['ctx'=16,'tp'=2] {'ctx'}, dimensions={0}, use_global_device_ids=true | all-gather | bytes 34816 | tf_op jit(solution)/shard_map/all_gather | solution.py:128
  188.9 39.5 %all-gather = f32[16,64,8]{1,2,0:T(8,128)S(1)} all-gather(f32[1,64,8]{1,2,0:T(8,128)S(1)} %bitcast.186), channel_id=1, replica_groups=mesh['ctx'=16,'tp'=2] {'ctx'}, dimensions={0}, use_global_device_ids=true | all-gather | bytes 34816 | tf_op jit(solution)/shard_map/all_gather | solution.py:127
  228.5 2.7 select_exponential_fusion
  232.5 3.3 %fusion.64 = bf16[8,8,8,128]{3,2,1,0:T(8,128)(2,1)S(1)} fusion(f32[8,1024,64]{1,2,0:T(8,128)} %copy-done.1, bf16[1024,8,128]{0,2,1:T(8,128)(2,1)S(1)} %bitcast.181, f32[8,1024]{1,0:T(8,128)S(1)} %bitcast.184, bf16[1024,1024]{1,0:T(8,128)(2,1)} %all-gather.8.cloned.1.call-done, bf16[64,1024]{1,0:T(8,128)(2,1)S(1)} %fusion.52), kind=kOutput, calls=%fused_computation.54 | convolution fusion | flops 270139392 | bytes 6586368 | tf_op jit(solution)/shard_map/hqk,qhd->khd/dot_general | solution.py:151
  235.9 2.5 fusion.10
  238.4 3.7 %fusion.68 = bf16[8,8,8,128]{3,2,1,0:T(8,128)(2,1)S(1)} fusion(bf16[1024,8,128]{0,2,1:T(8,128)(2,1)} %bitcast.182, f32[8,64,1024]{2,1,0:T(8,128)S(1)} %copy-done.3, f32[8,64]{1,0:T(8,128)S(1)} %bitcast.188, f32[8,64]{1,0:T(8,128)S(1)} %log_add_fusion, pred[64,1024]{1,0:T(8,128)(4,1)S(1)} %broadcast_compare_fusion.1, ...), kind=kOutput, calls=%fused_computation.56 | convolution fusion | flops 271712256 | bytes 6623232 | tf_op jit(solution)/shard_map/hqk,khd->qhd/dot_general | solution.py:123
  242.1 2.4 fusion.39
  244.5 3.1 %fusion.36 = f32[64,1024]{1,0:T(8,128)} fusion(f32[64,1024]{1,0:T(8,128)S(1)} %fusion.39, bf16[3,1024,1024]{2,1,0:T(8,128)(2,1)} %param.10, bf16[8,8,8,128]{3,2,1,0:T(8,128)(2,1)S(1)} %fusion.67), kind=kOutput, calls=%fused_computation.41 | convolution fusion | flops 134283264 | bytes 2752512 | tf_op jit(solution)/shard_map/dot_general | solution.py:162
  252.8 3.7 %reduce-scatter.2.cloned.1.call-done = f32[64,512]{1,0:T(8,128)} async-done(((f32[64,1024]{1,0:T(8,128)}), f32[64,512]{1,0:T(8,128)}) %reduce-scatter.2.cloned.1.call-update) | async-done | bytes 131088 | tf_op jit(solution)/shard_map/reduce_scatter | solution.py:165
  257.4 3.4 %collective-permute-start.17 = (bf16[64,512]{1,0:T(8,128)(2,1)S(1)}, bf16[64,512]{1,0:T(8,128)(2,1)S(1)}, u32[]{:S(2)}, u32[]{:S(2)}) collective-permute-start(bf16[64,512]{1,0:T(8,128)(2,1)S(1)} %convert_element_type.89), channel_id=1, source_target_pairs={{0,2},{2,4},{4,6},{6,8},{8,10},{10,12},{12,14},{14,16},{16,18},{18... | collective-permute-start | bytes 196616 | tf_op jit(solution)/shard_map/ppermute | solution.py:34
  260.8 2.5 collective-permute-start.18
  264.0 4.8 %collective-permute-done.18 = bf16[64,512]{1,0:T(8,128)(2,1)S(1)} collective-permute-done((bf16[64,512]{1,0:T(8,128)(2,1)S(1)}, bf16[64,512]{1,0:T(8,128)(2,1)S(1)}, u32[]{:S(2)}, u32[]{:S(2)}) %collective-permute-start.18) | collective-permute-done | bytes 65568 | tf_op jit(solution)/shard_map/ppermute | solution.py:35
  (167 shorter events, 37.1 us)
Async XLA Ops:
  7.2 121.1 %all-gather.10.cloned.1.call-start = ((), (), s32[]{:S(2)}) async-start(), calls=%async_computation.3 | async-start | bytes 2228224 | tf_op jit(solution)/shard_map/all_gather | solution.py:133
  7.9 140.4 %all-gather.6.cloned.1.call-start = ((), (), s32[]{:S(2)}) async-start(), calls=%async_computation.1 | async-start | bytes 2228224 | tf_op jit(solution)/shard_map/all_gather | solution.py:101
  8.8 10.9 %copy-start.30 = (f32[128]{0:T(128)}, f32[128]{0:T(128)S(1)}, u32[]{:S(2)}) copy-start(f32[128]{0:T(128)S(1)} %convert_reduce_fusion) | copy-start | bytes 1540
  9.7 14.6 %collective-permute-start = (bf16[128,512]{1,0:T(8,128)(2,1)S(1)}, bf16[128,512]{1,0:T(8,128)(2,1)S(1)}, u32[]{:S(2)}, u32[]{:S(2)}) collective-permute-start(bf16[128,512]{1,0:T(8,128)(2,1)S(1)} %fusion.48), channel_id=1, source_target_pairs={{0,2},{2,4},{4,6},{6,8},{8,10},{10,12},{12,14},{14,16},{16,18},{18... | collective-permute-start | bytes 393224 | tf_op jit(solution)/shard_map/ppermute | solution.py:34
  13.1 11.2 %collective-permute-start.1 = (bf16[128,512]{1,0:T(8,128)(2,1)S(1)}, bf16[128,512]{1,0:T(8,128)(2,1)S(1)}, u32[]{:S(2)}, u32[]{:S(2)}) collective-permute-start(bf16[128,512]{1,0:T(8,128)(2,1)S(1)} %fusion.48), channel_id=1, source_target_pairs={{2,0},{4,2},{6,4},{8,6},{10,8},{12,10},{14,12},{16,14},{18,16},{20... | collective-permute-start | bytes 393224 | tf_op jit(solution)/shard_map/ppermute | solution.py:35
  29.1 199.4 %all-gather.8.cloned.1.call-start = ((), (), s32[]{:S(2)}) async-start(), calls=%async_computation.2 | async-start | bytes 2228224 | tf_op jit(solution)/shard_map/all_gather | solution.py:132
  31.9 40.9 %copy-start.26 = (s32[16]{0:T(128)S(1)}, s32[16]{0:T(128)}, u32[]{:S(2)}) copy-start(s32[16]{0:T(128)} %param.8) | copy-start | bytes 196
  31.9 224.6 %reduce-scatter.2.cloned.1.call-start = ((), (), s32[]{:S(2)}) async-start(), calls=%async_computation.4 | async-start | bytes 393216 | tf_op jit(solution)/shard_map/reduce_scatter | solution.py:165
  34.1 8.5 %collective-permute-start.2 = (bf16[64,1024]{1,0:T(8,128)(2,1)S(1)}, bf16[64,1024]{1,0:T(8,128)(2,1)S(1)}, u32[]{:S(2)}, u32[]{:S(2)}) collective-permute-start(bf16[64,1024]{1,0:T(8,128)(2,1)S(1)} %fusion.52), channel_id=1, source_target_pairs={{0,2},{2,4},{4,6},{6,8},{8,10},{10,12},{12,14},{14,16},{16,18},{18... | collective-permute-start | bytes 393224 | tf_op jit(solution)/shard_map/ppermute | solution.py:17
  37.4 8.9 %collective-permute-start.3 = (bf16[64,1024]{1,0:T(8,128)(2,1)S(1)}, bf16[64,1024]{1,0:T(8,128)(2,1)S(1)}, u32[]{:S(2)}, u32[]{:S(2)}) collective-permute-start(bf16[64,1024]{1,0:T(8,128)(2,1)S(1)} %fusion.52), channel_id=1, source_target_pairs={{0,30},{2,0},{4,2},{6,4},{8,6},{10,8},{12,10},{14,12},{16,14},{18,... | collective-permute-start | bytes 393224 | tf_op jit(solution)/shard_map/ppermute | solution.py:20
  42.6 8.3 %collective-permute-start.4 = (bf16[64,1024]{1,0:T(8,128)(2,1)S(1)}, bf16[64,1024]{1,0:T(8,128)(2,1)S(1)}, u32[]{:S(2)}, u32[]{:S(2)}) collective-permute-start(bf16[64,1024]{1,0:T(8,128)(2,1)S(1)} %collective-permute-done.2), channel_id=1, source_target_pairs={{0,2},{2,4},{4,6},{6,8},{8,10},{10,12},{12,14},{14,16},{16,18},{18... | collective-permute-start | bytes 393224 | tf_op jit(solution)/shard_map/ppermute | solution.py:17
  46.3 8.9 %collective-permute-start.5 = (bf16[64,1024]{1,0:T(8,128)(2,1)S(1)}, bf16[64,1024]{1,0:T(8,128)(2,1)S(1)}, u32[]{:S(2)}, u32[]{:S(2)}) collective-permute-start(bf16[64,1024]{1,0:T(8,128)(2,1)S(1)} %collective-permute-done.3), channel_id=1, source_target_pairs={{0,30},{2,0},{4,2},{6,4},{8,6},{10,8},{12,10},{14,12},{16,14},{18,... | collective-permute-start | bytes 393224 | tf_op jit(solution)/shard_map/ppermute | solution.py:20
  50.9 6.8 %collective-permute-start.6 = (bf16[64,1024]{1,0:T(8,128)(2,1)S(1)}, bf16[64,1024]{1,0:T(8,128)(2,1)S(1)}, u32[]{:S(2)}, u32[]{:S(2)}) collective-permute-start(bf16[64,1024]{1,0:T(8,128)(2,1)S(1)} %collective-permute-done.4), channel_id=1, source_target_pairs={{0,2},{2,4},{4,6},{6,8},{8,10},{10,12},{12,14},{14,16},{16,18},{18... | collective-permute-start | bytes 393224 | tf_op jit(solution)/shard_map/ppermute | solution.py:17
  55.2 7.3 %collective-permute-start.7 = (bf16[64,1024]{1,0:T(8,128)(2,1)S(1)}, bf16[64,1024]{1,0:T(8,128)(2,1)S(1)}, u32[]{:S(2)}, u32[]{:S(2)}) collective-permute-start(bf16[64,1024]{1,0:T(8,128)(2,1)S(1)} %collective-permute-done.5), channel_id=1, source_target_pairs={{0,30},{2,0},{4,2},{6,4},{8,6},{10,8},{12,10},{14,12},{16,14},{18,... | collective-permute-start | bytes 393224 | tf_op jit(solution)/shard_map/ppermute | solution.py:20
  57.7 4.8 %copy-start.9 = (bf16[64,1024]{1,0:T(8,128)(2,1)}, bf16[64,1024]{1,0:T(8,128)(2,1)S(1)}, u32[]{:S(2)}) copy-start(bf16[64,1024]{1,0:T(8,128)(2,1)S(1)} %collective-permute-done.6) | copy-start | bytes 393220
  57.7 10.0 %collective-permute-start.8 = (bf16[64,1024]{1,0:T(8,128)(2,1)S(1)}, bf16[64,1024]{1,0:T(8,128)(2,1)S(1)}, u32[]{:S(2)}, u32[]{:S(2)}) collective-permute-start(bf16[64,1024]{1,0:T(8,128)(2,1)S(1)} %collective-permute-done.6), channel_id=1, source_target_pairs={{0,2},{2,4},{4,6},{6,8},{8,10},{10,12},{12,14},{14,16},{16,18},{18... | collective-permute-start | bytes 393224 | tf_op jit(solution)/shard_map/ppermute | solution.py:17
  62.5 31.7 %copy-start.11 = (bf16[64,1024]{1,0:T(8,128)(2,1)}, bf16[64,1024]{1,0:T(8,128)(2,1)S(1)}, u32[]{:S(2)}) copy-start(bf16[64,1024]{1,0:T(8,128)(2,1)S(1)} %collective-permute-done.7) | copy-start | bytes 393220
  62.5 10.5 %collective-permute-start.9 = (bf16[64,1024]{1,0:T(8,128)(2,1)S(1)}, bf16[64,1024]{1,0:T(8,128)(2,1)S(1)}, u32[]{:S(2)}, u32[]{:S(2)}) collective-permute-start(bf16[64,1024]{1,0:T(8,128)(2,1)S(1)} %collective-permute-done.7), channel_id=1, source_target_pairs={{0,30},{2,0},{4,2},{6,4},{8,6},{10,8},{12,10},{14,12},{16,14},{18,... | collective-permute-start | bytes 393224 | tf_op jit(solution)/shard_map/ppermute | solution.py:20
  67.7 26.5 %copy-start.13 = (bf16[64,1024]{1,0:T(8,128)(2,1)}, bf16[64,1024]{1,0:T(8,128)(2,1)S(1)}, u32[]{:S(2)}) copy-start(bf16[64,1024]{1,0:T(8,128)(2,1)S(1)} %collective-permute-done.8) | copy-start | bytes 393220
  67.7 8.7 %collective-permute-start.10 = (bf16[64,1024]{1,0:T(8,128)(2,1)S(1)}, bf16[64,1024]{1,0:T(8,128)(2,1)S(1)}, u32[]{:S(2)}, u32[]{:S(2)}) collective-permute-start(bf16[64,1024]{1,0:T(8,128)(2,1)S(1)} %collective-permute-done.8), channel_id=1, source_target_pairs={{0,2},{2,4},{4,6},{6,8},{8,10},{10,12},{12,14},{14,16},{16,18},{18... | collective-permute-start | bytes 393224 | tf_op jit(solution)/shard_map/ppermute | solution.py:17
  73.1 21.2 %copy-start.15 = (bf16[64,1024]{1,0:T(8,128)(2,1)}, bf16[64,1024]{1,0:T(8,128)(2,1)S(1)}, u32[]{:S(2)}) copy-start(bf16[64,1024]{1,0:T(8,128)(2,1)S(1)} %collective-permute-done.9) | copy-start | bytes 393220
  73.1 9.5 %collective-permute-start.11 = (bf16[64,1024]{1,0:T(8,128)(2,1)S(1)}, bf16[64,1024]{1,0:T(8,128)(2,1)S(1)}, u32[]{:S(2)}, u32[]{:S(2)}) collective-permute-start(bf16[64,1024]{1,0:T(8,128)(2,1)S(1)} %collective-permute-done.9), channel_id=1, source_target_pairs={{0,30},{2,0},{4,2},{6,4},{8,6},{10,8},{12,10},{14,12},{16,14},{18,... | collective-permute-start | bytes 393224 | tf_op jit(solution)/shard_map/ppermute | solution.py:20
  76.4 17.8 %copy-start.17 = (bf16[64,1024]{1,0:T(8,128)(2,1)}, bf16[64,1024]{1,0:T(8,128)(2,1)S(1)}, u32[]{:S(2)}) copy-start(bf16[64,1024]{1,0:T(8,128)(2,1)S(1)} %collective-permute-done.10) | copy-start | bytes 393220
  76.4 6.3 %collective-permute-start.12 = (bf16[64,1024]{1,0:T(8,128)(2,1)S(1)}, bf16[64,1024]{1,0:T(8,128)(2,1)S(1)}, u32[]{:S(2)}, u32[]{:S(2)}) collective-permute-start(bf16[64,1024]{1,0:T(8,128)(2,1)S(1)} %collective-permute-done.10), channel_id=1, source_target_pairs={{0,2},{2,4},{4,6},{6,8},{8,10},{10,12},{12,14},{14,16},{16,18},{18... | collective-permute-start | bytes 393224 | tf_op jit(solution)/shard_map/ppermute | solution.py:17
  82.5 11.7 %copy-start.19 = (bf16[64,1024]{1,0:T(8,128)(2,1)}, bf16[64,1024]{1,0:T(8,128)(2,1)S(1)}, u32[]{:S(2)}) copy-start(bf16[64,1024]{1,0:T(8,128)(2,1)S(1)} %collective-permute-done.11) | copy-start | bytes 393220
  82.5 7.7 %collective-permute-start.13 = (bf16[64,1024]{1,0:T(8,128)(2,1)S(1)}, bf16[64,1024]{1,0:T(8,128)(2,1)}, u32[]{:S(2)}, u32[]{:S(2)}) collective-permute-start(bf16[64,1024]{1,0:T(8,128)(2,1)S(1)} %collective-permute-done.11), channel_id=1, source_target_pairs={{0,30},{2,0},{4,2},{6,4},{8,6},{10,8},{12,10},{14,12},{16,14},{18,... | collective-permute-start | bytes 393224 | tf_op jit(solution)/shard_map/ppermute | solution.py:20
  82.7 11.5 %copy-start.21 = (bf16[64,1024]{1,0:T(8,128)(2,1)}, bf16[64,1024]{1,0:T(8,128)(2,1)S(1)}, u32[]{:S(2)}) copy-start(bf16[64,1024]{1,0:T(8,128)(2,1)S(1)} %collective-permute-done.12) | copy-start | bytes 393220
  82.7 8.3 %collective-permute-start.14 = (bf16[64,1024]{1,0:T(8,128)(2,1)S(1)}, bf16[64,1024]{1,0:T(8,128)(2,1)}, u32[]{:S(2)}, u32[]{:S(2)}) collective-permute-start(bf16[64,1024]{1,0:T(8,128)(2,1)S(1)} %collective-permute-done.12), channel_id=1, source_target_pairs={{0,2},{2,4},{4,6},{6,8},{8,10},{10,12},{12,14},{14,16},{16,18},{18... | collective-permute-start | bytes 393224 | tf_op jit(solution)/shard_map/ppermute | solution.py:17
  90.3 31.2 %collective-permute-start.15 = (bf16[64,1024]{1,0:T(8,128)(2,1)}, bf16[64,1024]{1,0:T(8,128)(2,1)}, u32[]{:S(2)}, u32[]{:S(2)}) collective-permute-start(bf16[64,1024]{1,0:T(8,128)(2,1)} %collective-permute-done.13), channel_id=1, source_target_pairs={{0,30},{2,0},{4,2},{6,4},{8,6},{10,8},{12,10},{14,12},{16,14},{18,... | collective-permute-start | bytes 393224 | tf_op jit(solution)/shard_map/ppermute | solution.py:20
  91.0 32.7 %collective-permute-start.16 = (bf16[64,1024]{1,0:T(8,128)(2,1)}, bf16[64,1024]{1,0:T(8,128)(2,1)}, u32[]{:S(2)}, u32[]{:S(2)}) collective-permute-start(bf16[64,1024]{1,0:T(8,128)(2,1)} %collective-permute-done.14), channel_id=1, source_target_pairs={{0,2},{2,4},{4,6},{6,8},{8,10},{10,12},{12,14},{14,16},{16,18},{18... | collective-permute-start | bytes 393224 | tf_op jit(solution)/shard_map/ppermute | solution.py:17
  96.9 4.8 %copy-start.8 = (bf16[64,1024]{1,0:T(8,128)(2,1)S(1)}, bf16[64,1024]{1,0:T(8,128)(2,1)}, u32[]{:S(2)}) copy-start(bf16[64,1024]{1,0:T(8,128)(2,1)} %copy-done.7) | copy-start | bytes 393220
  98.3 5.7 %copy-start.10 = (bf16[64,1024]{1,0:T(8,128)(2,1)S(1)}, bf16[64,1024]{1,0:T(8,128)(2,1)}, u32[]{:S(2)}) copy-start(bf16[64,1024]{1,0:T(8,128)(2,1)} %copy-done.9) | copy-start | bytes 393220
  99.7 5.7 %copy-start.12 = (bf16[64,1024]{1,0:T(8,128)(2,1)S(1)}, bf16[64,1024]{1,0:T(8,128)(2,1)}, u32[]{:S(2)}) copy-start(bf16[64,1024]{1,0:T(8,128)(2,1)} %copy-done.11) | copy-start | bytes 393220
  101.9 4.8 %copy-start.14 = (bf16[64,1024]{1,0:T(8,128)(2,1)S(1)}, bf16[64,1024]{1,0:T(8,128)(2,1)}, u32[]{:S(2)}) copy-start(bf16[64,1024]{1,0:T(8,128)(2,1)} %copy-done.13) | copy-start | bytes 393220
  104.1 4.7 %copy-start.16 = (bf16[64,1024]{1,0:T(8,128)(2,1)S(1)}, bf16[64,1024]{1,0:T(8,128)(2,1)}, u32[]{:S(2)}) copy-start(bf16[64,1024]{1,0:T(8,128)(2,1)} %copy-done.15) | copy-start | bytes 393220
  105.5 5.5 %copy-start.18 = (bf16[64,1024]{1,0:T(8,128)(2,1)S(1)}, bf16[64,1024]{1,0:T(8,128)(2,1)}, u32[]{:S(2)}) copy-start(bf16[64,1024]{1,0:T(8,128)(2,1)} %copy-done.17) | copy-start | bytes 393220
  106.9 5.3 %copy-start.20 = (bf16[64,1024]{1,0:T(8,128)(2,1)S(1)}, bf16[64,1024]{1,0:T(8,128)(2,1)}, u32[]{:S(2)}) copy-start(bf16[64,1024]{1,0:T(8,128)(2,1)} %copy-done.19) | copy-start | bytes 393220
  109.0 4.6 %copy-start.22 = (bf16[64,1024]{1,0:T(8,128)(2,1)S(1)}, bf16[64,1024]{1,0:T(8,128)(2,1)}, u32[]{:S(2)}) copy-start(bf16[64,1024]{1,0:T(8,128)(2,1)} %copy-done.21) | copy-start | bytes 393220
  128.3 20.0 %copy-start.6 = (bf16[64,1024]{1,0:T(8,128)(2,1)S(1)}, bf16[64,1024]{1,0:T(8,128)(2,1)}, u32[]{:S(2)}) copy-start(bf16[64,1024]{1,0:T(8,128)(2,1)} %fusion.55) | copy-start | bytes 393220
  150.9 4.0 %copy-start.2 = (f32[8,64,1024]{2,1,0:T(8,128)}, f32[8,64,1024]{2,1,0:T(8,128)S(1)}, u32[]{:S(2)}) copy-start(f32[8,64,1024]{2,1,0:T(8,128)S(1)} %get-tuple-element.16) | copy-start | bytes 6291460
  153.3 75.2 %copy-start.24 = (bf16[64,1024]{1,0:T(8,128)(2,1)S(1)}, bf16[64,1024]{1,0:T(8,128)(2,1)}, u32[]{:S(2)}) copy-start(bf16[64,1024]{1,0:T(8,128)(2,1)} %fusion.58) | copy-start | bytes 393220
  244.4 4.5 %copy-start.28 = (s32[1,16]{1,0:T(1,128)S(1)}, s32[1,16]{1,0:T(1,128)}, u32[]{:S(2)}) copy-start(s32[1,16]{1,0:T(1,128)} %get-tuple-element.4) | copy-start | bytes 196
  244.4 4.5 %copy-start.29 = (s32[1,16]{1,0:T(1,128)S(1)}, s32[1,16]{1,0:T(1,128)}, u32[]{:S(2)}) copy-start(s32[1,16]{1,0:T(1,128)} %get-tuple-element.6) | copy-start | bytes 196
  244.4 7.7 %copy-start.27 = (s32[256]{0:T(256)S(1)}, s32[256]{0:T(256)}, u32[]{:S(2)}) copy-start(s32[256]{0:T(256)} %param.7) | copy-start | bytes 3076
  244.4 7.7 %copy-start.31 = (f32[128]{0:T(128)S(1)}, f32[128]{0:T(128)}, u32[]{:S(2)}) copy-start(f32[128]{0:T(128)} %copy-done.30) | copy-start | bytes 1540
  244.5 18.8 %copy-start.25 = (bf16[8,128,64]{1,2,0:T(8,128)(2,1)S(1)}, bf16[8,128,64]{1,2,0:T(8,128)(2,1)}, u32[]{:S(2)}) copy-start(bf16[8,128,64]{1,2,0:T(8,128)(2,1)} %get-tuple-element.18) | copy-start | bytes 393220
  257.4 6.5 %collective-permute-start.17 = (bf16[64,512]{1,0:T(8,128)(2,1)S(1)}, bf16[64,512]{1,0:T(8,128)(2,1)S(1)}, u32[]{:S(2)}, u32[]{:S(2)}) collective-permute-start(bf16[64,512]{1,0:T(8,128)(2,1)S(1)} %convert_element_type.89), channel_id=1, source_target_pairs={{0,2},{2,4},{4,6},{6,8},{8,10},{10,12},{12,14},{14,16},{16,18},{18... | collective-permute-start | bytes 196616 | tf_op jit(solution)/shard_map/ppermute | solution.py:34
  260.8 8.0 %collective-permute-start.18 = (bf16[64,512]{1,0:T(8,128)(2,1)S(1)}, bf16[64,512]{1,0:T(8,128)(2,1)S(1)}, u32[]{:S(2)}, u32[]{:S(2)}) collective-permute-start(bf16[64,512]{1,0:T(8,128)(2,1)S(1)} %convert_element_type.89), channel_id=1, source_target_pairs={{2,0},{4,2},{6,4},{8,6},{10,8},{12,10},{14,12},{16,14},{18,16},{20... | collective-permute-start | bytes 196616 | tf_op jit(solution)/shard_map/ppermute | solution.py:35
  (7 other events, 14.9 us)
Sparse Core Ops, SparseCore 0:
  10.8 74.0 all-gather.9
  87.6 60.6 all-gather.5
  151.1 59.5 all-gather.7
  247.7 8.7 reduce-scatter.1
